TPU v7x, 128 devices: a whole 4x4x4 slice. The times are simulated.
128 devices in a mesh: group: 32 (over z, y, core), local: 4 (over x).
Axes of the slice: x: 4, y: 4, z: 4, core: 2. Of those that a mesh axis runs over, the one named last changes fastest.
Arguments:
- dense_vec: bfloat16 [16384, 128], P(('group', 'local')), may hold values from -6 to 6
- q_tables: float32 [4096, 26, 128], P('group'), may hold values from -4 to 4
- r_tables: float32 [256, 26, 128], P('local'), may hold values from -4 to 4
- owner: int32 [16384, 26, 1], P(('group', 'local')), may hold values from 0 to 31; in each aligned block of 3328 rows (0 to 3327, 3328 to 6655, ..., all dimensions but the last counted through in order) at most 208 rows name the same one
- q_local: int32 [16384, 26], P(('group', 'local')), may hold values from 0 to 127
- r_index: int32 [16384, 26], P(('group', 'local')), may hold values from 0 to 255
- w_one: bfloat16 [479, 1024], replicated, may hold values from -0.25 to 0.25
- b_one: float32 [1024], replicated, may hold values from -3 to 3
- w_two: bfloat16 [1024, 1024], replicated, may hold values from -0.1875 to 0.1875
- b_two: float32 [1024], replicated, may hold values from -3 to 3
- w_three: bfloat16 [1024, 512], replicated, may hold values from -0.1875 to 0.1875
- b_three: float32 [512], replicated, may hold values from -3 to 3
- w_four: bfloat16 [512, 256], replicated, may hold values from -0.25 to 0.25
- b_four: float32 [256], replicated, may hold values from -3 to 3
- cotangent: bfloat16 [16384, 256], P(('group', 'local')), may hold values from -6 to 6
Outputs:
- q_new: float32 [4096, 26, 128], P('group')
- r_new: float32 [256, 26, 128], P('local')
- w_one_new: float32 [479, 1024], replicated
- b_one_new: float32 [1024], replicated
- w_two_new: float32 [1024, 1024], replicated
- b_two_new: float32 [1024], replicated
- w_three_new: float32 [1024, 512], replicated
- b_three_new: float32 [512], replicated
- w_four_new: float32 [512, 256], replicated
- b_four_new: float32 [256], replicated
Inputs may be any that keep to these rules, and one draw needn't show every extreme that they name: `owner`: within the rows of one device (its 128 samples times 26 tables), no group is named more than 208 times, a bound that some block reaches.
All inputs are finite; a program needn't handle non-finite values.
Results may differ from a plain program's by a relative error of at most 0.0025.
Values may be sent and summed in bfloat16 or wider, within the bound.
No kernel may reach another device: no remote copies, remote signals or barrier semaphores. Data moves between devices by JAX's collectives and lax.ppermute only.
A program may use at most 128 MiB of HBM per device.

v0:
```python
import jax
import jax.numpy as jnp
import numpy as np
from jax import lax
from jax.sharding import PartitionSpec as P

table_rate = 0.05
dense_rate = 0.0005


def cut_along(array, dim, length):
    before, after = (array.shape[:dim], array.shape[dim + 1 :])
    return jnp.moveaxis(array.reshape(*before, length, -1, *after), dim, 0)


def summed_on_arrival(array, axis, dim):
    blocks = cut_along(array, dim, lax.axis_size(axis))
    arrived = lax.all_to_all(blocks, axis, split_axis=0, concat_axis=0, tiled=True)
    return arrived.astype(jnp.float32).sum(axis=0)


def in_order(blocks, dim):
    shape = list(blocks.shape[1:])
    shape[dim] *= blocks.shape[0]
    return jnp.moveaxis(blocks, 0, dim).reshape(shape)


def sent_to_all(array, axis):
    length = lax.axis_size(axis)
    return lax.all_to_all(
        jnp.broadcast_to(array[None], (length, *array.shape)), axis, 0, 0, tiled=True
    )


def gather_directly(array, axis, dim):
    return in_order(sent_to_all(array, axis), dim)


def silu_slope(preact):
    sigma = jax.nn.sigmoid(preact)
    return sigma * (1.0 + preact * (1.0 - sigma))


def interact(dense_rows, embeds):
    vectors_all = jnp.concatenate([dense_rows[:, None, :], embeds], axis=1).astype(jnp.float32)
    gram_mat = jnp.einsum("bid,bjd->bij", vectors_all, vectors_all, precision=lax.Precision.HIGHEST)
    lower_i, lower_j = np.tril_indices(vectors_all.shape[1], -1)
    pair_vals = gram_mat[:, lower_i, lower_j]
    features = jnp.concatenate([dense_rows.astype(jnp.float32), pair_vals], axis=1).astype(
        jnp.bfloat16
    )
    return (vectors_all, features)


def pair_back(d_pairs, vectors_all):
    vectors = vectors_all.shape[1]
    lower_i, lower_j = np.tril_indices(vectors, -1)
    spread = (
        jnp.zeros((vectors_all.shape[0], vectors, vectors), jnp.float32)
        .at[:, lower_i, lower_j]
        .set(d_pairs)
    )
    spread = spread + jnp.swapaxes(spread, 1, 2)
    return jnp.einsum("bij,bjd->bid", spread, vectors_all, precision=lax.Precision.HIGHEST)


def contract_rows(left, right):
    return lax.dot_general(
        left, right, (((0,), (0,)), ((), ())), preferred_element_type=jnp.float32
    )


def dense_pass(features, layers, cot_rows):
    inputs_list = [features]
    pre_list = []
    current = features
    for layer_idx, (weight, biases) in enumerate(layers):
        pre_act = jnp.dot(current, weight, preferred_element_type=jnp.float32) + biases
        pre_list.append(pre_act)
        if layer_idx + 1 < len(layers):
            current = jax.nn.silu(pre_act).astype(jnp.bfloat16)
            inputs_list.append(current)
    grad_low = cot_rows
    grad_full = cot_rows.astype(jnp.float32)
    grads = []
    back_grad = None
    for layer_idx in reversed(range(len(layers))):
        weight = layers[layer_idx][0]
        w_grad = contract_rows(inputs_list[layer_idx], grad_low)
        b_grad = jnp.sum(grad_full, axis=0)
        back_grad = lax.dot_general(
            grad_low, weight, (((1,), (1,)), ((), ())), preferred_element_type=jnp.float32
        )
        grads.insert(0, (w_grad, b_grad))
        if layer_idx > 0:
            grad_full = back_grad * silu_slope(pre_list[layer_idx - 1])
            grad_low = grad_full.astype(jnp.bfloat16)
    return (grads, back_grad)


def body(
    dense_vec,
    q_tables,
    r_tables,
    owner,
    q_local,
    r_index,
    w_one,
    b_one,
    w_two,
    b_two,
    w_three,
    b_three,
    w_four,
    b_four,
    cotangent,
):
    layers = [(w_one, b_one), (w_two, b_two), (w_three, b_three), (w_four, b_four)]
    groups = lax.axis_size("group")
    batch_rows, table_count = q_local.shape
    embed_width = q_tables.shape[2]
    lookups = batch_rows * table_count
    capacity = 2 * lookups // groups
    slot_count = groups * capacity
    segment_count = q_tables.shape[0] * table_count
    table_ids = jnp.arange(table_count, dtype=jnp.int32)[None, :]
    highest = lax.Precision.HIGHEST
    dest_group = owner[:, :, 0]
    owner_hits = (
        dest_group[:, :, None] == jnp.arange(groups, dtype=jnp.int32)[None, None, :]
    ).astype(jnp.float32)
    table_lower = (jnp.arange(table_count)[:, None] < jnp.arange(table_count)[None, :]).astype(
        jnp.float32
    )
    sample_lower = (jnp.arange(batch_rows)[:, None] < jnp.arange(batch_rows)[None, :]).astype(
        jnp.float32
    )
    within = jnp.einsum("st,bsg->btg", table_lower, owner_hits, precision=highest)
    before = jnp.einsum("cb,cg->bg", sample_lower, jnp.sum(owner_hits, axis=1), precision=highest)
    slot_rank = jnp.sum((within + before[:, None, :]) * owner_hits, axis=2).astype(jnp.int32)
    position = (dest_group * capacity + slot_rank).reshape(lookups)
    source = (
        jnp.full((slot_count,), lookups, jnp.int32)
        .at[position]
        .set(jnp.arange(lookups, dtype=jnp.int32))
    )
    row_keys = (q_local * table_count + table_ids).reshape(lookups)
    keys_padded = jnp.concatenate([row_keys, jnp.zeros((1,), jnp.int32)])
    outgoing = keys_padded[source].reshape(groups, capacity)
    flat_table = q_tables.reshape(segment_count, embed_width)
    request = lax.all_to_all(outgoing, "group", split_axis=0, concat_axis=0, tiled=True)
    served_rows = flat_table[request].astype(jnp.bfloat16)
    arrived = lax.all_to_all(served_rows, "group", split_axis=0, concat_axis=0, tiled=True)
    q_rows = arrived.reshape(slot_count, embed_width)[position]
    full_r = lax.all_gather(r_tables, "local", axis=0, tiled=True)
    remainder_count = full_r.shape[0]
    r_pick = (
        r_index[:, :, None] == jnp.arange(remainder_count, dtype=jnp.int32)[None, None, :]
    ).astype(jnp.float32)
    r_rows = jnp.einsum("btr,rtd->btd", r_pick, full_r, precision=highest).reshape(
        lookups, embed_width
    )
    q_val = q_rows.astype(jnp.float32)
    embeds = (q_val * r_rows).astype(jnp.bfloat16).reshape(batch_rows, table_count, embed_width)
    vectors_all, features = interact(dense_vec, embeds)
    grads, d_features = dense_pass(features, layers, cotangent)
    d_embed = pair_back(d_features[:, embed_width:], vectors_all)[:, 1:, :].reshape(
        lookups, embed_width
    )
    grad_padded = jnp.concatenate(
        [d_embed * r_rows, jnp.zeros((1, embed_width), jnp.float32)], axis=0
    )
    outbound = grad_padded[source].reshape(groups, capacity, embed_width)
    returned = (
        lax.all_to_all(
            outbound.astype(jnp.bfloat16), "group", split_axis=0, concat_axis=0, tiled=True
        )
        .astype(outbound.dtype)
        .reshape(slot_count, embed_width)
    )
    served_flat = request.reshape(slot_count)
    q_part = jax.ops.segment_sum(returned, served_flat, num_segments=segment_count).reshape(
        q_tables.shape
    )
    q_piece = summed_on_arrival(q_part.astype(jnp.bfloat16), "local", 0)
    quarter = q_piece.shape[0]
    own_rows = lax.dynamic_slice_in_dim(q_tables, lax.axis_index("local") * quarter, quarter, 0)
    q_new = gather_directly(own_rows - table_rate * q_piece, "local", 0)
    r_part = jnp.einsum(
        "btr,btd->rtd",
        r_pick,
        (d_embed * q_val).reshape(batch_rows, table_count, embed_width),
        precision=highest,
    )
    summed = lax.psum(r_part, ("group", "local"))
    r_grad = lax.dynamic_slice_in_dim(
        summed, lax.axis_index("local") * r_tables.shape[0], r_tables.shape[0], 0
    )
    r_new = r_tables - table_rate * r_grad
    grad_wa, grad_ba, grad_wb, grad_bb, grad_wc, grad_bc, grad_wd, grad_bd = lax.psum(
        (
            grads[0][0],
            grads[0][1],
            grads[1][0],
            grads[1][1],
            grads[2][0],
            grads[2][1],
            grads[3][0],
            grads[3][1],
        ),
        ("group", "local"),
    )
    summed_grads = [(grad_wa, grad_ba), (grad_wb, grad_bb), (grad_wc, grad_bc), (grad_wd, grad_bd)]
    updated = []
    for (weight, biases), (w_grad, b_grad) in zip(layers, summed_grads):
        updated.append(weight.astype(jnp.float32) - dense_rate * w_grad)
        updated.append(biases - dense_rate * b_grad)
    return (
        q_new,
        r_new,
        updated[0],
        updated[1],
        updated[2],
        updated[3],
        updated[4],
        updated[5],
        updated[6],
        updated[7],
    )


def solution(mesh):
    return jax.shard_map(
        body,
        mesh=mesh,
        in_specs=(
            P(("group", "local"), None),
            P("group", None, None),
            P("local", None, None),
            P(("group", "local"), None, None),
            P(("group", "local"), None),
            P(("group", "local"), None),
            P(),
            P(),
            P(),
            P(),
            P(),
            P(),
            P(),
            P(),
            P(("group", "local"), None),
        ),
        out_specs=(
            P("group", None, None),
            P("local", None, None),
            P(),
            P(),
            P(),
            P(),
            P(),
            P(),
            P(),
            P(),
        ),
        check_vma=False,
    )
```

profile of v0, /device:TPU:1, one launch (start us, length us, event | category | flops | bytes accessed | tf_op | source)
XLA Modules:
  0.0 415.2 jit_solution(16516317859253861610)
XLA Ops:
  11.4 12.8 %scatter_custom_fusion = s32[6656]{0:T(1024)S(1)} fusion(s32[3328]{0:T(1024)S(1)} %fusion.39, s32[3328]{0:T(1024)S(1)} %iota.29, s32[]{:T(128)} %constant.27.clone.1), kind=kCustom, calls=%fused_computation.86 | custom fusion | bytes 26628 | tf_op jit(solution)/shard_map/scatter | solution.py:145
  24.2 34.5 %gather_fusion = s32[6656]{0:T(1024)S(1)} fusion(s32[3329]{0:T(1024)S(1)} %pad_add_fusion, s32[7168]{0:T(1024)S(1)} %pad_clamp_fusion.1), kind=kCustom, calls=%fused_computation | custom fusion | bytes 79872 | tf_op jit(solution)/shard_map/gather | solution.py:149
  59.5 9.6 %all-to-all-start = ((s32[32,1,208]{2,1,0:T(1,128)}), s32[32,1,208]{2,1,0:T(1,128)S(1)}, u32[]{:S(2)}, u32[]{:S(2)}) async-start(s32[32,1,208]{2,1,0:T(1,128)} %all_to_all.20), calls=%async_computation | async-start | bytes 65536 | tf_op jit(solution)/shard_map/all_to_all | solution.py:151
  71.8 4.6 %all-to-all-done = s32[32,1,208]{2,1,0:T(1,128)S(1)} async-done(((s32[32,1,208]{2,1,0:T(1,128)}), s32[32,1,208]{2,1,0:T(1,128)S(1)}, u32[]{:S(2)}, u32[]{:S(2)}) %all-to-all-start) | async-done | bytes 26656 | tf_op jit(solution)/shard_map/all_to_all | solution.py:151
  76.6 14.3 %gather_fusion.1 = bf16[6656,128]{1,0:T(8,128)(2,1)} fusion(bf16[3328,128]{1,0:T(8,128)(2,1)S(1)} %reshape.133, s32[7168]{0:T(1024)S(1)} %pad_clamp_fusion), kind=kCustom, calls=%fused_computation.1 | custom fusion | bytes 3434496 | tf_op jit(solution)/shard_map/gather | solution.py:152
  90.8 4.2 %all-to-all-start.1 = ((bf16[32,208,128]{2,1,0:T(8,128)(2,1)}), bf16[32,208,128]{2,1,0:T(8,128)(2,1)S(1)}, u32[]{:S(2)}, u32[]{:S(2)}) async-start(bf16[32,208,128]{2,1,0:T(8,128)(2,1)} %bitcast.56), calls=%async_computation.1 | async-start | bytes 3407872 | tf_op jit(solution)/shard_map/all_to_all | solution.py:153
  95.4 24.1 %all-to-all-done.1 = bf16[32,208,128]{2,1,0:T(8,128)(2,1)S(1)} async-done(((bf16[32,208,128]{2,1,0:T(8,128)(2,1)}), bf16[32,208,128]{2,1,0:T(8,128)(2,1)S(1)}, u32[]{:S(2)}, u32[]{:S(2)}) %all-to-all-start.1) | async-done | bytes 1703968 | tf_op jit(solution)/shard_map/all_to_all | solution.py:153
  119.5 6.5 %gather_fusion.2 = bf16[3328,128]{1,0:T(8,128)(2,1)S(1)} fusion(bf16[6656,128]{1,0:T(8,128)(2,1)S(1)} %bitcast.54, s32[4096]{0:T(1024)S(1)} %pad_clamp_fusion.2), kind=kCustom, calls=%fused_computation.2 | custom fusion | bytes 1717248 | tf_op jit(solution)/shard_map/gather | solution.py:154
  126.7 7.3 %fusion.5 = (bf16[128,26,128]{2,0,1:T(8,128)(2,1)S(1)}, f32[26,128,128]{2,1,0:T(8,128)}) fusion(f32[128,26,128]{2,1,0:T(8,128)S(1)} %reshape.138, f32[256,26,128]{2,0,1:T(8,128)} %all-gather.2.cloned.1.call-done, s32[128,26]{0,1:T(8,128)S(1)} %copy-done.15), kind=kOutput, calls=%fused_computation.19 | convolution fusion | flops 1310326784 | bytes 7681024 | tf_op jit(solution)/shard_map/btr,rtd->btd/dot_general | solution.py:160
  135.9 4.9 %gather_fusion.3 = bf16[351,128]{1,0:T(8,128)(2,1)S(1)} fusion(bf16[128,27,27]{0,2,1:T(8,128)(2,1)S(1)} %copy.92, s32[351]{0:T(512)S(1)} %copy-done), kind=kCustom, calls=%fused_computation.3 | custom fusion | bytes 182520 | tf_op jit(solution)/shard_map/gather | solution.py:48
  156.3 19.0 %scatter_fusion = f32[128,27,27]{0,2,1:T(8,128)S(1)} fusion(f32[128,27,27]{0,2,1:T(8,128)S(1)} %broadcast_in_dim.23, s32[351]{0:T(512)S(1)} %copy-done, f32[351,128]{1,0:T(8,128)S(1)} %convolution_bitcast_fusion), kind=kCustom, calls=%fused_computation.6 | custom fusion | bytes 541944 | tf_op jit(solution)/shard_map/scatter | solution.py:61
  175.6 2.9 copy.111
  178.5 3.3 fusion.14
  181.9 6.2 %fusion.4 = f32[256,26,128]{0,2,1:T(8,128)} fusion(s32[128,26]{0,1:T(8,128)S(1)} %copy-done.15, f32[128,26,128]{2,1,0:T(8,128)S(1)} %fusion.14, f32[128,26,128]{2,1,0:T(8,128)S(1)} %copy-done.2), kind=kOutput, calls=%fused_computation.16 | convolution fusion | flops 1309900800 | bytes 6829056 | tf_op jit(solution)/shard_map/btr,btd->rtd/dot_general | solution.py:189
  191.5 14.2 %gather_fusion.4 = bf16[6656,128]{1,0:T(8,128)(2,1)} fusion(bf16[3329,128]{1,0:T(8,128)(2,1)S(1)} %concatenate.24, s32[7168]{0:T(1024)S(1)} %pad_clamp_fusion.1), kind=kCustom, calls=%fused_computation.4 | custom fusion | bytes 3434496 | tf_op jit(solution)/shard_map/gather | solution.py:173
  205.8 5.0 %all-to-all-start.2 = ((bf16[32,208,128]{2,1,0:T(8,128)(2,1)}), bf16[32,208,128]{2,1,0:T(8,128)(2,1)S(1)}, u32[]{:S(2)}, u32[]{:S(2)}) async-start(bf16[32,208,128]{2,1,0:T(8,128)(2,1)} %bitcast.10), calls=%async_computation.2 | async-start | bytes 3407872 | tf_op jit(solution)/shard_map/all_to_all | solution.py:175
  210.9 28.2 %all-to-all-done.2 = bf16[32,208,128]{2,1,0:T(8,128)(2,1)S(1)} async-done(((bf16[32,208,128]{2,1,0:T(8,128)(2,1)}), bf16[32,208,128]{2,1,0:T(8,128)(2,1)S(1)}, u32[]{:S(2)}, u32[]{:S(2)}) %all-to-all-start.2) | async-done | bytes 1703968 | tf_op jit(solution)/shard_map/all_to_all | solution.py:175
  239.2 40.3 %scatter_custom_fusion.2 = f32[3328,128]{1,0:T(8,128)S(1)} fusion(s32[6656]{0:T(1024)S(1)} %reshape.195, bf16[6656,128]{1,0:T(8,128)(2,1)S(1)} %bitcast.55, f32[]{:T(128)} %constant.24.clone.1), kind=kCustom, calls=%fused_computation.9 | custom fusion | flops 1703936 | bytes 3407876 | tf_op jit(solution)/shard_map/scatter-add | solution.py:182
  283.0 4.2 %all-to-all-start.3 = ((bf16[4,32,26,128]{3,1,2,0:T(8,128)(2,1)}), bf16[4,32,26,128]{3,1,2,0:T(8,128)(2,1)S(1)}, u32[]{:S(2)}, u32[]{:S(2)}) async-start(bf16[4,32,26,128]{3,1,2,0:T(8,128)(2,1)} %copy.99), calls=%async_computation.3 | async-start | bytes 1703936 | tf_op jit(solution)/shard_map/all_to_all | solution.py:18
  287.3 13.2 %all-to-all-done.3 = bf16[4,32,26,128]{3,1,2,0:T(8,128)(2,1)S(1)} async-done(((bf16[4,32,26,128]{3,1,2,0:T(8,128)(2,1)}), bf16[4,32,26,128]{3,1,2,0:T(8,128)(2,1)S(1)}, u32[]{:S(2)}, u32[]{:S(2)}) %all-to-all-start.3) | async-done | bytes 852000 | tf_op jit(solution)/shard_map/all_to_all | solution.py:18
  303.5 3.6 all-to-all-start.4
  308.8 82.5 %all-reduce.1 = (f32[1024]{0:T(1024)S(1)}, f32[1024]{0:T(1024)S(1)}, f32[512]{0:T(512)S(1)}, f32[256]{0:T(256)S(1)}) all-reduce(f32[1024]{0:T(1024)S(1)} %get-tuple-element.61, f32[1024]{0:T(1024)S(1)} %get-tuple-element.63, f32[512]{0:T(512)S(1)} %get-tuple-element.65, ...), channel_id=1, replica_groups=mesh['group'=32,'local'=4] {'group','local'}, use_global_device_ids=true, to_apply=%region_9.10 | all-reduce | flops 2816 | bytes 22528 | tf_op jit(solution)/shard_map/psum | solution.py:200
  397.8 3.4 multiply_subtract_fusion.2
  401.2 4.5 %multiply_subtract_fusion = f32[1024,1024]{1,0:T(8,128)} fusion(f32[1024,1024]{1,0:T(8,128)S(1)} %copy-done.4, bf16[1024,1024]{1,0:T(8,128)(2,1)} %param.31), kind=kLoop, calls=%fused_computation.8 | loop fusion | flops 3145728 | bytes 10485760 | tf_op jit(solution)/shard_map/sub | solution.py:216
  (116 shorter events, 47.2 us)
Async XLA Ops:
  7.2 119.1 %all-gather.2.cloned.1.call-start = ((), (), s32[]{:S(2)}) async-start(), calls=%async_computation.5 | async-start | bytes 4259840 | tf_op jit(solution)/shard_map/all_gather | solution.py:155
  59.5 16.9 %all-to-all-start = ((s32[32,1,208]{2,1,0:T(1,128)}), s32[32,1,208]{2,1,0:T(1,128)S(1)}, u32[]{:S(2)}, u32[]{:S(2)}) async-start(s32[32,1,208]{2,1,0:T(1,128)} %all_to_all.20), calls=%async_computation | async-start | bytes 65536 | tf_op jit(solution)/shard_map/all_to_all | solution.py:151
  71.6 19.3 %copy-start.3 = (f32[128,26,128]{2,1,0:T(8,128)}, f32[128,26,128]{2,1,0:T(8,128)S(1)}, u32[]{:S(2)}) copy-start(f32[128,26,128]{2,1,0:T(8,128)S(1)} %copy.84) | copy-start | bytes 5111812
  90.8 4.4 %copy-start.14 = (bf16[128,128]{1,0:T(8,128)(2,1)S(1)}, bf16[128,128]{1,0:T(8,128)(2,1)}, u32[]{:S(2)}) copy-start(bf16[128,128]{1,0:T(8,128)(2,1)} %param.23) | copy-start | bytes 98308
  90.8 28.7 %all-to-all-start.1 = ((bf16[32,208,128]{2,1,0:T(8,128)(2,1)}), bf16[32,208,128]{2,1,0:T(8,128)(2,1)S(1)}, u32[]{:S(2)}, u32[]{:S(2)}) async-start(bf16[32,208,128]{2,1,0:T(8,128)(2,1)} %bitcast.56), calls=%async_computation.1 | async-start | bytes 3407872 | tf_op jit(solution)/shard_map/all_to_all | solution.py:153
  95.0 299.4 %all-reduce.5.cloned.1.call-start = ((), (), s32[]{:S(2)}) async-start(), calls=%async_computation.6 | async-start | bytes 24379392 | tf_op jit(solution)/shard_map/psum | solution.py:195
  126.2 7.8 %copy-start.1 = (f32[128,26,128]{2,1,0:T(8,128)}, f32[128,26,128]{2,1,0:T(8,128)S(1)}, u32[]{:S(2)}) copy-start(f32[128,26,128]{2,1,0:T(8,128)S(1)} %reshape.138) | copy-start | bytes 5111812
  134.1 1.8 copy-start
  134.1 6.7 %copy-start.17 = (f32[1024]{0:T(1024)S(1)}, f32[1024]{0:T(1024)}, u32[]{:S(2)}) copy-start(f32[1024]{0:T(1024)} %param.30) | copy-start | bytes 12292
  134.8 7.6 %copy-start.18 = (f32[1024]{0:T(1024)S(1)}, f32[1024]{0:T(1024)}, u32[]{:S(2)}) copy-start(f32[1024]{0:T(1024)} %param.32) | copy-start | bytes 12292
  142.4 2.2 copy-start.9
  142.4 2.2 copy-start.19
  145.8 1.6 copy-start.7
  178.5 3.4 copy-start.2
  205.8 33.4 %all-to-all-start.2 = ((bf16[32,208,128]{2,1,0:T(8,128)(2,1)}), bf16[32,208,128]{2,1,0:T(8,128)(2,1)S(1)}, u32[]{:S(2)}, u32[]{:S(2)}) async-start(bf16[32,208,128]{2,1,0:T(8,128)(2,1)} %bitcast.10), calls=%async_computation.2 | async-start | bytes 3407872 | tf_op jit(solution)/shard_map/all_to_all | solution.py:175
  283.0 17.4 %all-to-all-start.3 = ((bf16[4,32,26,128]{3,1,2,0:T(8,128)(2,1)}), bf16[4,32,26,128]{3,1,2,0:T(8,128)(2,1)S(1)}, u32[]{:S(2)}, u32[]{:S(2)}) async-start(bf16[4,32,26,128]{3,1,2,0:T(8,128)(2,1)} %copy.99), calls=%async_computation.3 | async-start | bytes 1703936 | tf_op jit(solution)/shard_map/all_to_all | solution.py:18
  303.5 89.5 %all-to-all-start.4 = ((f32[4,32,26,128]{3,1,2,0:T(8,128)}), f32[4,32,26,128]{3,1,2,0:T(8,128)S(1)}, u32[]{:S(2)}, u32[]{:S(2)}) async-start(f32[4,32,26,128]{3,1,2,0:T(8,128)} %broadcast_in_dim.29), calls=%async_computation.4 | async-start | bytes 3407872 | tf_op jit(solution)/shard_map/all_to_all | solution.py:30
  307.1 84.2 %copy-start.20 = (f32[256]{0:T(256)S(1)}, f32[256]{0:T(256)}, u32[]{:S(2)}) copy-start(f32[256]{0:T(256)} %param.36) | copy-start | bytes 3076
  396.4 1.4 copy-start.6
  397.8 3.4 copy-start.4
  401.2 4.5 %copy-start.8 = (f32[1024,512]{1,0:T(8,128)S(1)}, f32[1024,512]{1,0:T(8,128)}, u32[]{:S(2)}) copy-start(f32[1024,512]{1,0:T(8,128)} %get-tuple-element.57) | copy-start | bytes 6291460
  401.2 4.5 %copy-start.10 = (bf16[1024,512]{1,0:T(8,128)(2,1)S(1)}, bf16[1024,512]{1,0:T(8,128)(2,1)}, u32[]{:S(2)}) copy-start(bf16[1024,512]{1,0:T(8,128)(2,1)} %param.33) | copy-start | bytes 3145732
  405.8 1.7 copy-start.11
  405.8 1.7 copy-start.13
  (4 other events, 3.8 us)
Sparse Core Ops, SparseCore 0:
  9.6 44.6 all-gather.1
  188.2 188.2 all-reduce.4
where the time goes:
time: 416 us; the launch traced here: 415 us
  local copies, waits for them, and re-layouts  128 us (31%)
  blocking collectives  82.5 us (20%)
  waiting for transfers between devices  70.8 us (17%)
  other arithmetic  61.5 us (15%)
  matrix products  31.2 us (8%)
  starting transfers between devices  26.8 us (6%)
  between operations  14.6 us (4%)
    psum x1, blocking collectives, body(): lax.psum((grads[0][0], grads[0][1], grads[1][0], grads[1][1], grads[2][0]...  82.5 us
    scatter-add x1, other arithmetic, body(): jax.ops.segment_sum(returned, served_flat, num_segments=segment_count)  40.3 us
    gather x1, local copies, waits for them, and re-layouts, body(): outgoing = keys_padded[source].reshape(groups, capacity)  34.5 us
    all_to_all x1, waiting for transfers between devices, body(): lax.all_to_all(outbound.astype(jnp.bfloat16), 'group', split_axis=0, conc...  28.2 us
    all_to_all x1, waiting for transfers between devices, body(): lax.all_to_all(served_rows, 'group', split_axis=0, concat_axis=0, tiled=T...  24.1 us
    scatter x1, local copies, waits for them, and re-layouts, pair_back(): spread = jnp.zeros((vectors_all.shape[0], vectors, vectors), jnp.float32)...  19 us
    gather x1, local copies, waits for them, and re-layouts, body(): served_rows = flat_table[request].astype(jnp.bfloat16)  14.3 us
    gather x1, local copies, waits for them, and re-layouts, body(): outbound = grad_padded[source].reshape(groups, capacity, embed_width)  14.2 us
  transfers between devices with their start and end apart: 7, of which 4 were waited for; matrix products, arithmetic and copies ran while one was open for 35% of the time, Pallas kernels for 0%

commit v1 on v0

--- a/solution.py
+++ b/solution.py
@@ -198,17 +198,20 @@
     )
     r_new = r_tables - table_rate * r_grad
     grad_wa, grad_ba, grad_wb, grad_bb, grad_wc, grad_bc, grad_wd, grad_bd = lax.psum(
-        (
-            grads[0][0],
-            grads[0][1],
-            grads[1][0],
-            grads[1][1],
-            grads[2][0],
-            grads[2][1],
-            grads[3][0],
-            grads[3][1],
+        lax.psum(
+            (
+                grads[0][0],
+                grads[0][1],
+                grads[1][0],
+                grads[1][1],
+                grads[2][0],
+                grads[2][1],
+                grads[3][0],
+                grads[3][1],
+            ),
+            "local",
         ),
-        ("group", "local"),
+        "group",
     )
     summed_grads = [(grad_wa, grad_ba), (grad_wb, grad_bb), (grad_wc, grad_bc), (grad_wd, grad_bd)]
     updated = []

time: 416 us -> 638 us (1.53)
  waiting for transfers between devices: 70.8 us -> 227 us
  blocking collectives: 82.5 us -> 148 us
    psum x0 -> x2, waiting for transfers between devices: none -> 161 us  [the longest x1 132 us: body(): lax.psum((grads[0][0], grads[0][1], grads[1][0], grads[1][1], grads[2][0]...]
    psum x0 -> x1, blocking collectives: none -> 120 us  [body(): lax.psum(lax.psum((grads[0][0], grads[0][1], grads[1][0], grads[1][1], gr...]
    psum x1, blocking collectives: 82.5 us -> 27.4 us  [body(): lax.psum((grads[0][0], grads[0][1], grads[1][0], grads[1][1], grads[2][0]...]
  transfers between devices with their start and end apart: 7 -> 9, of which waited for: 4 -> 6; matrix products, arithmetic and copies ran while one was open for 35% -> 28% of each run, Pallas kernels for 0% -> 0%
where the time goes in v1:
time: 638 us; the launch traced here: 637 us
  waiting for transfers between devices  227 us (36%)
  blocking collectives  148 us (23%)
  local copies, waits for them, and re-layouts  128 us (20%)
  other arithmetic  60.1 us (9%)
  starting transfers between devices  30.2 us (5%)
  matrix products  30 us (5%)
  between operations  14.4 us (2%)
    psum x1, waiting for transfers between devices, body(): lax.psum((grads[0][0], grads[0][1], grads[1][0], grads[1][1], grads[2][0]...  132 us
    psum x1, blocking collectives, body(): lax.psum(lax.psum((grads[0][0], grads[0][1], grads[1][0], grads[1][1], gr...  120 us
    scatter-add x1, other arithmetic, body(): jax.ops.segment_sum(returned, served_flat, num_segments=segment_count)  40.6 us
    gather x1, local copies, waits for them, and re-layouts, body(): outgoing = keys_padded[source].reshape(groups, capacity)  34.5 us
    psum x1, waiting for transfers between devices, body(): lax.psum(lax.psum((grads[0][0], grads[0][1], grads[1][0], grads[1][1], gr...  28.6 us
    psum x1, blocking collectives, body(): lax.psum((grads[0][0], grads[0][1], grads[1][0], grads[1][1], grads[2][0]...  27.4 us
    all_to_all x1, waiting for transfers between devices, body(): lax.all_to_all(outbound.astype(jnp.bfloat16), 'group', split_axis=0, conc...  26.3 us
    all_to_all x1, waiting for transfers between devices, body(): lax.all_to_all(served_rows, 'group', split_axis=0, concat_axis=0, tiled=T...  24.1 us
  transfers between devices with their start and end apart: 9, of which 6 were waited for; matrix products, arithmetic and copies ran while one was open for 28% of the time, Pallas kernels for 0%

profile of v1, /device:TPU:1, one launch (start us, length us, event | category | flops | bytes accessed | tf_op | source)
XLA Modules:
  0.0 637.3 jit_solution(2615601814701471318)
XLA Ops:
  11.4 12.8 %scatter_custom_fusion = s32[6656]{0:T(1024)S(1)} fusion(s32[3328]{0:T(1024)S(1)} %fusion.39, s32[3328]{0:T(1024)S(1)} %iota.29, s32[]{:T(128)} %constant.27.clone.1), kind=kCustom, calls=%fused_computation.86 | custom fusion | bytes 26628 | tf_op jit(solution)/shard_map/scatter | solution.py:145
  24.2 34.5 %gather_fusion = s32[6656]{0:T(1024)S(1)} fusion(s32[3329]{0:T(1024)S(1)} %pad_add_fusion, s32[7168]{0:T(1024)S(1)} %pad_clamp_fusion.1), kind=kCustom, calls=%fused_computation | custom fusion | bytes 79872 | tf_op jit(solution)/shard_map/gather | solution.py:149
  59.5 9.6 %all-to-all-start = ((s32[32,1,208]{2,1,0:T(1,128)}), s32[32,1,208]{2,1,0:T(1,128)S(1)}, u32[]{:S(2)}, u32[]{:S(2)}) async-start(s32[32,1,208]{2,1,0:T(1,128)} %all_to_all.20), calls=%async_computation | async-start | bytes 65536 | tf_op jit(solution)/shard_map/all_to_all | solution.py:151
  71.8 4.6 all-to-all-done
  76.6 14.3 %gather_fusion.1 = bf16[6656,128]{1,0:T(8,128)(2,1)} fusion(bf16[3328,128]{1,0:T(8,128)(2,1)S(1)} %reshape.133, s32[7168]{0:T(1024)S(1)} %pad_clamp_fusion), kind=kCustom, calls=%fused_computation.1 | custom fusion | bytes 3434496 | tf_op jit(solution)/shard_map/gather | solution.py:152
  90.8 4.2 all-to-all-start.1
  95.4 24.1 %all-to-all-done.1 = bf16[32,208,128]{2,1,0:T(8,128)(2,1)S(1)} async-done(((bf16[32,208,128]{2,1,0:T(8,128)(2,1)}), bf16[32,208,128]{2,1,0:T(8,128)(2,1)S(1)}, u32[]{:S(2)}, u32[]{:S(2)}) %all-to-all-start.1) | async-done | bytes 1703968 | tf_op jit(solution)/shard_map/all_to_all | solution.py:153
  119.5 6.5 %gather_fusion.2 = bf16[3328,128]{1,0:T(8,128)(2,1)S(1)} fusion(bf16[6656,128]{1,0:T(8,128)(2,1)S(1)} %bitcast.54, s32[4096]{0:T(1024)S(1)} %pad_clamp_fusion.2), kind=kCustom, calls=%fused_computation.2 | custom fusion | bytes 1717248 | tf_op jit(solution)/shard_map/gather | solution.py:154
  126.7 7.3 %fusion.5 = (bf16[128,26,128]{2,0,1:T(8,128)(2,1)S(1)}, f32[26,128,128]{2,1,0:T(8,128)}) fusion(f32[128,26,128]{2,1,0:T(8,128)S(1)} %reshape.138, f32[256,26,128]{2,0,1:T(8,128)} %all-gather.2.cloned.1.call-done, s32[128,26]{0,1:T(8,128)S(1)} %copy-done.17), kind=kOutput, calls=%fused_computation.19 | convolution fusion | flops 1310326784 | bytes 7681024 | tf_op jit(solution)/shard_map/btr,rtd->btd/dot_general | solution.py:160
  135.9 4.9 gather_fusion.3
  155.1 18.8 %scatter_fusion = f32[128,27,27]{0,2,1:T(8,128)S(1)} fusion(f32[128,27,27]{0,2,1:T(8,128)S(1)} %broadcast_in_dim.23, s32[351]{0:T(512)S(1)} %copy-done, f32[351,128]{1,0:T(8,128)S(1)} %convolution_bitcast_fusion), kind=kCustom, calls=%fused_computation.6 | custom fusion | bytes 541944 | tf_op jit(solution)/shard_map/scatter | solution.py:61
  180.4 6.2 fusion.4
  186.7 132.2 %all-reduce.13.cloned.1.call-done = (f32[479,1024]{1,0:T(8,128)}, f32[1024,1024]{1,0:T(8,128)}, f32[1024,512]{1,0:T(8,128)}, f32[512,256]{1,0:T(8,128)}) async-done(((f32[479,1024]{1,0:T(8,128)}, f32[1024,1024]{1,0:T(8,128)}, f32[1024,512]{1,0:T(8,128)}, f32[512,256]{1,0:T(8,128)}), (f32[479,1024]{1,0:T(8,128)}, f32[1024,1024]{1,0:T(8,128)}, f32[1024,512]{1,0:T(8,128)}, ...) | async-done | bytes 8777744 | tf_op jit(solution)/shard_map/psum | solution.py:201
  322.3 14.2 %gather_fusion.4 = bf16[6656,128]{1,0:T(8,128)(2,1)} fusion(bf16[3329,128]{1,0:T(8,128)(2,1)S(1)} %concatenate.24, s32[7168]{0:T(1024)S(1)} %pad_clamp_fusion.1), kind=kCustom, calls=%fused_computation.4 | custom fusion | bytes 3434496 | tf_op jit(solution)/shard_map/gather | solution.py:173
  336.5 7.9 %all-to-all-start.2 = ((bf16[32,208,128]{2,1,0:T(8,128)(2,1)}), bf16[32,208,128]{2,1,0:T(8,128)(2,1)S(1)}, u32[]{:S(2)}, u32[]{:S(2)}) async-start(bf16[32,208,128]{2,1,0:T(8,128)(2,1)} %bitcast.10), calls=%async_computation.2 | async-start | bytes 3407872 | tf_op jit(solution)/shard_map/all_to_all | solution.py:175
  344.6 26.3 %all-to-all-done.2 = bf16[32,208,128]{2,1,0:T(8,128)(2,1)S(1)} async-done(((bf16[32,208,128]{2,1,0:T(8,128)(2,1)}), bf16[32,208,128]{2,1,0:T(8,128)(2,1)S(1)}, u32[]{:S(2)}, u32[]{:S(2)}) %all-to-all-start.2) | async-done | bytes 1703968 | tf_op jit(solution)/shard_map/all_to_all | solution.py:175
  370.9 40.6 %scatter_custom_fusion.2 = f32[3328,128]{1,0:T(8,128)S(1)} fusion(s32[6656]{0:T(1024)S(1)} %reshape.195, bf16[6656,128]{1,0:T(8,128)(2,1)S(1)} %bitcast.55, f32[]{:T(128)} %constant.24.clone.1), kind=kCustom, calls=%fused_computation.9 | custom fusion | flops 1703936 | bytes 3407876 | tf_op jit(solution)/shard_map/scatter-add | solution.py:182
  415.0 3.5 all-to-all-start.3
  418.5 10.7 %all-to-all-done.3 = bf16[4,32,26,128]{3,1,2,0:T(8,128)(2,1)S(1)} async-done(((bf16[4,32,26,128]{3,1,2,0:T(8,128)(2,1)}), bf16[4,32,26,128]{3,1,2,0:T(8,128)(2,1)S(1)}, u32[]{:S(2)}, u32[]{:S(2)}) %all-to-all-start.3) | async-done | bytes 852000 | tf_op jit(solution)/shard_map/all_to_all | solution.py:18
  432.3 4.5 all-to-all-start.4
  437.4 27.4 %all-reduce.3 = (f32[1024]{0:T(1024)S(1)}, f32[1024]{0:T(1024)S(1)}, f32[512]{0:T(512)S(1)}, f32[256]{0:T(256)S(1)}) all-reduce(f32[1024]{0:T(1024)S(1)} %get-tuple-element.68, f32[1024]{0:T(1024)S(1)} %get-tuple-element.70, f32[512]{0:T(512)S(1)} %get-tuple-element.72, ...), channel_id=1, replica_groups=mesh['group'=32,'local'=4] {'local'}, use_global_device_ids=true, to_apply=%region_10.11 | all-reduce | flops 2816 | bytes 22528 | tf_op jit(solution)/shard_map/psum | solution.py:201
  464.8 120.4 %all-reduce.1 = (f32[1024]{0:T(1024)S(1)}, f32[1024]{0:T(1024)S(1)}, f32[512]{0:T(512)S(1)}, f32[256]{0:T(256)S(1)}) all-reduce(f32[1024]{0:T(1024)S(1)} %get-tuple-element.58, f32[1024]{0:T(1024)S(1)} %get-tuple-element.59, f32[512]{0:T(512)S(1)} %get-tuple-element.60, ...), channel_id=1, replica_groups=mesh['group'=32,'local'=4] {'group'}, use_global_device_ids=true, to_apply=%region_11.12 | all-reduce | flops 2816 | bytes 22528 | tf_op jit(solution)/shard_map/psum | solution.py:200
  593.3 28.6 %all-reduce.11.cloned.1.call-done = (f32[479,1024]{1,0:T(8,128)}, f32[1024,1024]{1,0:T(8,128)}, f32[1024,512]{1,0:T(8,128)}, f32[512,256]{1,0:T(8,128)}) async-done(((f32[479,1024]{1,0:T(8,128)}, f32[1024,1024]{1,0:T(8,128)}, f32[1024,512]{1,0:T(8,128)}, f32[512,256]{1,0:T(8,128)}), (f32[479,1024]{1,0:T(8,128)}, f32[1024,1024]{1,0:T(8,128)}, f32[1024,512]{1,0:T(8,128)}, ...) | async-done | bytes 8777744 | tf_op jit(solution)/shard_map/psum | solution.py:200
  621.9 3.4 multiply_subtract_fusion.2
  (127 shorter events, 55.5 us)
Async XLA Ops:
  7.2 119.1 %all-gather.2.cloned.1.call-start = ((), (), s32[]{:S(2)}) async-start(), calls=%async_computation.5 | async-start | bytes 4259840 | tf_op jit(solution)/shard_map/all_gather | solution.py:155
  59.5 16.9 %all-to-all-start = ((s32[32,1,208]{2,1,0:T(1,128)}), s32[32,1,208]{2,1,0:T(1,128)S(1)}, u32[]{:S(2)}, u32[]{:S(2)}) async-start(s32[32,1,208]{2,1,0:T(1,128)} %all_to_all.20), calls=%async_computation | async-start | bytes 65536 | tf_op jit(solution)/shard_map/all_to_all | solution.py:151
  71.6 19.3 %copy-start.3 = (f32[128,26,128]{2,1,0:T(8,128)}, f32[128,26,128]{2,1,0:T(8,128)S(1)}, u32[]{:S(2)}) copy-start(f32[128,26,128]{2,1,0:T(8,128)S(1)} %copy.84) | copy-start | bytes 5111812
  90.8 4.4 copy-start.16
  90.8 28.7 %all-to-all-start.1 = ((bf16[32,208,128]{2,1,0:T(8,128)(2,1)}), bf16[32,208,128]{2,1,0:T(8,128)(2,1)S(1)}, u32[]{:S(2)}, u32[]{:S(2)}) async-start(bf16[32,208,128]{2,1,0:T(8,128)(2,1)} %bitcast.56), calls=%async_computation.1 | async-start | bytes 3407872 | tf_op jit(solution)/shard_map/all_to_all | solution.py:153
  95.0 223.9 %all-reduce.13.cloned.1.call-start = ((), (), s32[]{:S(2)}) async-start(), calls=%async_computation.8 | async-start | bytes 17563648 | tf_op jit(solution)/shard_map/psum | solution.py:201
  126.2 7.8 %copy-start.1 = (f32[128,26,128]{2,1,0:T(8,128)}, f32[128,26,128]{2,1,0:T(8,128)S(1)}, u32[]{:S(2)}) copy-start(f32[128,26,128]{2,1,0:T(8,128)S(1)} %reshape.138) | copy-start | bytes 5111812
  134.1 6.7 %copy-start.5 = (bf16[479,1024]{1,0:T(8,128)(2,1)S(1)}, bf16[479,1024]{1,0:T(8,128)(2,1)}, u32[]{:S(2)}) copy-start(bf16[479,1024]{1,0:T(8,128)(2,1)} %param.29) | copy-start | bytes 2942980
  134.1 6.7 %copy-start.19 = (f32[1024]{0:T(1024)S(1)}, f32[1024]{0:T(1024)}, u32[]{:S(2)}) copy-start(f32[1024]{0:T(1024)} %param.30) | copy-start | bytes 12292
  134.8 6.4 copy-start.20
  141.2 2.2 copy-start.11
  154.4 432.6 %all-reduce.9.cloned.1.call-start = ((), (), s32[]{:S(2)}) async-start(), calls=%async_computation.6 | async-start | bytes 6815744 | tf_op jit(solution)/shard_map/psum | solution.py:195
  177.1 3.4 copy-start.2
  186.7 435.2 %all-reduce.11.cloned.1.call-start = ((), (), s32[]{:S(2)}) async-start(), calls=%async_computation.7 | async-start | bytes 17563648 | tf_op jit(solution)/shard_map/psum | solution.py:200
  336.5 34.3 %all-to-all-start.2 = ((bf16[32,208,128]{2,1,0:T(8,128)(2,1)}), bf16[32,208,128]{2,1,0:T(8,128)(2,1)S(1)}, u32[]{:S(2)}, u32[]{:S(2)}) async-start(bf16[32,208,128]{2,1,0:T(8,128)(2,1)} %bitcast.10), calls=%async_computation.2 | async-start | bytes 3407872 | tf_op jit(solution)/shard_map/all_to_all | solution.py:175
  415.0 14.3 %all-to-all-start.3 = ((bf16[4,32,26,128]{3,1,2,0:T(8,128)(2,1)}), bf16[4,32,26,128]{3,1,2,0:T(8,128)(2,1)S(1)}, u32[]{:S(2)}, u32[]{:S(2)}) async-start(bf16[4,32,26,128]{3,1,2,0:T(8,128)(2,1)} %copy.99), calls=%async_computation.3 | async-start | bytes 1703936 | tf_op jit(solution)/shard_map/all_to_all | solution.py:18
  432.3 4.5 copy-start.7
  432.3 158.0 %all-to-all-start.4 = ((f32[4,32,26,128]{3,1,2,0:T(8,128)}), f32[4,32,26,128]{3,1,2,0:T(8,128)}, u32[]{:S(2)}, u32[]{:S(2)}) async-start(f32[4,32,26,128]{3,1,2,0:T(8,128)} %broadcast_in_dim.29), calls=%async_computation.4 | async-start | bytes 3407872 | tf_op jit(solution)/shard_map/all_to_all | solution.py:30
  436.9 148.4 %copy-start.22 = (f32[256]{0:T(256)S(1)}, f32[256]{0:T(256)}, u32[]{:S(2)}) copy-start(f32[256]{0:T(256)} %param.36) | copy-start | bytes 3076
  590.3 31.6 %copy-start.6 = (bf16[479,1024]{1,0:T(8,128)(2,1)S(1)}, bf16[479,1024]{1,0:T(8,128)(2,1)}, u32[]{:S(2)}) copy-start(bf16[479,1024]{1,0:T(8,128)(2,1)} %param.29) | copy-start | bytes 2942980
  590.4 35.0 %copy-start.9 = (bf16[1024,1024]{1,0:T(8,128)(2,1)S(1)}, bf16[1024,1024]{1,0:T(8,128)(2,1)}, u32[]{:S(2)}) copy-start(bf16[1024,1024]{1,0:T(8,128)(2,1)} %param.31) | copy-start | bytes 6291460
  621.9 3.4 copy-start.4
  625.4 2.8 copy-start.10
  625.4 2.8 copy-start.12
  (8 other events, 11.6 us)
Sparse Core Ops, SparseCore 0:
  9.6 44.6 all-gather.1
  154.5 164.2 all-reduce.12
  323.8 174.6 all-reduce.8
  502.2 119.6 all-reduce.10
